TPU v7x, 128 devices: a whole 4x4x4 slice. The times are simulated.
128 devices in a mesh: dp: 1, hp: 2 (over core), cp: 64 (over z, y, x).
Axes of the slice: x: 4, y: 4, z: 4, core: 2. Of those that a mesh axis runs over, the one named last changes fastest.
Arguments:
- latent: bfloat16 [1536, 12, 128, 128], P(('dp', 'cp'), 'hp')
- conv_w: bfloat16 [4, 3, 3, 3, 128, 128], replicated
- conv_b: float32 [4, 128], replicated
- gn_gamma: float32 [4, 128], replicated
- gn_beta: float32 [4, 128], replicated
Outputs:
- output: bfloat16 [1536, 12, 128, 128], P(('dp', 'cp'), 'hp')
All inputs are finite; a program needn't handle non-finite values.
Results may differ from a plain program's by a relative error of at most 0.0101423.
Values are sent between devices in bfloat16 or wider.
A program may use at most 1 GiB of HBM per device.

v0:
```python
import jax
import jax.numpy as jnp
from jax import lax
from jax.sharding import PartitionSpec as P

GROUPS = 32
EPS = 1e-6


def norm_silu(local_act, gamma, beta, total_count):
    frames, row_count, lat_width, channels = local_act.shape
    per_group = channels // GROUPS
    grouped = local_act.reshape(frames, row_count, lat_width, GROUPS, per_group).astype(jnp.float32)
    stat_sums = jnp.stack([jnp.sum(grouped, axis=(0, 1, 2, 4)), jnp.sum(grouped * grouped, axis=(0, 1, 2, 4))])
    stat_sums = lax.psum(stat_sums, ("cp", "hp"))
    mean_val = stat_sums[0] / total_count
    variance = stat_sums[1] / total_count - mean_val * mean_val
    inv_std = lax.rsqrt(variance + EPS)
    gamma_g = gamma.reshape(GROUPS, per_group)
    scale_c = (inv_std[:, None] * gamma_g).reshape(channels)
    shift_c = (beta.reshape(GROUPS, per_group) - (mean_val * inv_std)[:, None] * gamma_g).reshape(channels)
    return jax.nn.silu(local_act.astype(jnp.float32) * scale_c + shift_c).astype(jnp.bfloat16)


def conv_valid(padded, kernel, bias_vec):
    conv_out = lax.conv_general_dilated(padded[None], kernel, (1, 1, 1), ((0, 0), (0, 0), (1, 1)), dimension_numbers=("NDHWC", "DHWIO", "NDHWC"), preferred_element_type=jnp.float32)
    return (conv_out[0] + bias_vec).astype(jnp.bfloat16)


def solution(mesh):
    n_time = mesh.shape["cp"]
    n_rows = mesh.shape["hp"]
    time_fwd = [(i, i + 1) for i in range(n_time - 1)]
    rows_down = [(i, i + 1) for i in range(n_rows - 1)]
    rows_up = [(i + 1, i) for i in range(n_rows - 1)]

    def local_decode(local_lat, conv_w, conv_b, gn_gamma, gn_beta):
        frames, row_count, lat_width, channels = local_lat.shape
        total_count = frames * n_time * row_count * n_rows * lat_width * (channels // GROUPS)
        time_rank = lax.axis_index("cp")
        residual = local_lat
        for block_idx in range(2):
            hidden = residual
            for sub_idx in range(2):
                layer_idx = 2 * block_idx + sub_idx
                activated = norm_silu(hidden, gn_gamma[layer_idx], gn_beta[layer_idx], total_count)
                prev_frames = lax.ppermute(activated[frames - 2:], "cp", time_fwd)
                own_first = jnp.broadcast_to(activated[:1], prev_frames.shape)
                prev_frames = jnp.where(time_rank == 0, own_first, prev_frames)
                extended = jnp.concatenate([prev_frames, activated], axis=0)
                from_above = lax.ppermute(extended[:, row_count - 1:], "hp", rows_down)
                from_below = lax.ppermute(extended[:, :1], "hp", rows_up)
                extended = jnp.concatenate([from_above, extended, from_below], axis=1)
                hidden = conv_valid(extended, conv_w[layer_idx], conv_b[layer_idx])
            residual = (residual.astype(jnp.float32) + hidden.astype(jnp.float32)).astype(jnp.bfloat16)
        return residual

    video_spec = P(("dp", "cp"), "hp", None, None)
    return jax.shard_map(local_decode, mesh=mesh, in_specs=(video_spec, P(), P(), P(), P()), out_specs=video_spec, check_vma=False)
```

profile of v0, /device:TPU:1, one launch (start us, length us, event | category | flops | bytes accessed | tf_op | source)
XLA Modules:
  0.0 745.9 jit_solution(13963327883235791389)
XLA Ops:
  0.0 7.3 convert_reduce_fusion.1
  7.7 68.7 %psum.28 = f32[2,32]{1,0:T(2,128)S(1)} all-reduce(f32[2,32]{1,0:T(2,128)S(1)} %pad_maximum_fusion.8), channel_id=1, replica_groups=mesh['dp'=1,'hp'=2,'cp'=64] {'cp','hp'}, use_global_device_ids=true, to_apply=%region_4.5 | all-reduce | flops 64 | bytes 512 | tf_op jit(solution)/shard_map/psum | solution.py:15
  77.5 6.4 fusion.11
  89.6 9.5 %collective-permute-done = bf16[2,6,128,128]{3,1,2,0:T(8,128)(2,1)S(1)} collective-permute-done((bf16[2,6,128,128]{3,1,2,0:T(8,128)(2,1)S(1)}, bf16[2,6,128,128]{3,1,2,0:T(8,128)(2,1)S(1)}, u32[]{:S(2)}, u32[]{:S(2)}) %collective-permute-start) | collective-permute-done | bytes 393248 | tf_op jit(solution)/shard_map/ppermute | solution.py:47
  99.1 7.3 pad_maximum_fusion.7
  116.4 7.0 maximum_bitcast_fusion
  132.7 41.5 %fusion.30 = (f32[128]{0:T(128)S(1)}, f32[128]{0:T(128)S(1)}, f32[24,6,8,17,128]{4,2,3,1,0:T(8,128)}) fusion(pred[8,17]{0,1:T(8,128)(4,1)S(1)} %copy-done.6, f32[128]{0:T(128)S(1)} %get-tuple-element.32, bf16[4,3,3,3,128,128]{5,4,3,2,1,0:T(8,128)(2,1)} %param.6, bf16[26,8,1,7,2,128]{5,3,4,1,0,2:T(8,128)(2,1)S(1)} %slice.170, ...), kind=kOutput, calls=%fused_computation.49 | convolution fusion | flops 17373511680 | bytes 18900616 | tf_op jit(solution)/shard_map/conv_general_dilated | solution.py:26
  174.6 69.7 %psum.29 = f32[2,32]{1,0:T(2,128)S(1)} all-reduce(f32[2,32]{1,0:T(2,128)S(1)} %pad_maximum_fusion.9), channel_id=1, replica_groups=mesh['dp'=1,'hp'=2,'cp'=64] {'cp','hp'}, use_global_device_ids=true, to_apply=%region_9.10 | all-reduce | flops 64 | bytes 512 | tf_op jit(solution)/shard_map/psum | solution.py:15
  244.7 7.1 copy.31
  251.8 4.2 slice.171
  256.0 10.7 %multiply_convert_fusion.1 = bf16[24,6,128,128]{3,1,2,0:T(8,128)(2,1)S(1)} fusion(f32[24,6,1,128,128]{4,0,3,1,2:T(8,128)} %slice.171, f32[128]{0:T(128)S(1)} %get-tuple-element.39, f32[128]{0:T(128)S(1)} %get-tuple-element.38, f32[128]{0:T(128)S(1)} %get-tuple-element.32), kind=kLoop, calls=%fused_computation.44 | loop fusion | flops 23592960 | bytes 14157312 | tf_op jit(solution)/shard_map/convert_element_type | solution.py:22
  268.5 10.5 %collective-permute-done.3 = bf16[2,6,128,128]{3,1,2,0:T(8,128)(2,1)S(1)} collective-permute-done((bf16[2,6,128,128]{3,1,2,0:T(8,128)(2,1)S(1)}, bf16[2,6,128,128]{3,1,2,0:T(8,128)(2,1)S(1)}, u32[]{:S(2)}, u32[]{:S(2)}) %collective-permute-start.3) | collective-permute-done | bytes 393248 | tf_op jit(solution)/shard_map/ppermute | solution.py:47
  292.7 7.2 maximum_bitcast_fusion.1
  309.2 41.1 %broadcast_select_fusion.2 = f32[24,6,8,17,128]{4,2,3,1,0:T(8,128)} fusion(pred[8,17]{0,1:T(8,128)(4,1)S(1)} %copy-done.6, bf16[26,8,1,7,2,128]{5,3,4,1,0,2:T(8,128)(2,1)S(1)} %slice.174, bf16[26,8,1,8,17,128]{5,3,4,1,0,2:T(8,128)(2,1)} %copy.38, bf16[4,3,3,3,128,128]{5,4,3,2,1,0:T(8,128)(2,1)} %param.6), kind=kOutput, calls=%fused_computation.87 | convolution fusion | flops 17353457664 | bytes 18899080 | tf_op jit(solution)/shard_map/conv_general_dilated | solution.py:26
  350.3 7.1 copy.39
  357.3 4.2 slice.175
  361.6 15.0 %convert_reduce_fusion = (f32[128]{0:T(128)S(1)}, f32[128]{0:T(128)S(1)}, bf16[24,6,128,128]{3,1,2,0:T(8,128)(2,1)}) fusion(f32[128]{0:T(128)S(1)} %get-tuple-element.31, f32[24,6,1,128,128]{4,0,3,1,2:T(8,128)} %slice.175, bf16[24,6,128,128]{3,2,1,0:T(8,128)(2,1)S(1)} %bitcast.204), kind=kLoop, calls=%fused_computation.3 | loop fusion | flops 23592704 | bytes 18875904 | tf_op jit(solution)/shard_map/reduce_sum | solution.py:14
  377.1 69.8 %psum.30 = f32[2,32]{1,0:T(2,128)S(1)} all-reduce(f32[2,32]{1,0:T(2,128)S(1)} %pad_maximum_fusion.10), channel_id=1, replica_groups=mesh['dp'=1,'hp'=2,'cp'=64] {'cp','hp'}, use_global_device_ids=true, to_apply=%region_14.15 | all-reduce | flops 64 | bytes 512 | tf_op jit(solution)/shard_map/psum | solution.py:15
  447.3 5.7 fusion.20
  454.4 10.5 %collective-permute-done.6 = bf16[2,6,128,128]{3,1,2,0:T(8,128)(2,1)S(1)} collective-permute-done((bf16[2,6,128,128]{3,1,2,0:T(8,128)(2,1)S(1)}, bf16[2,6,128,128]{3,1,2,0:T(8,128)(2,1)S(1)}, u32[]{:S(2)}, u32[]{:S(2)}) %collective-permute-start.6) | collective-permute-done | bytes 393248 | tf_op jit(solution)/shard_map/ppermute | solution.py:47
  478.6 7.4 maximum_bitcast_fusion.2
  495.4 41.4 %fusion.33 = (f32[128]{0:T(128)S(1)}, f32[128]{0:T(128)S(1)}, f32[24,6,8,17,128]{4,2,3,1,0:T(8,128)}) fusion(pred[8,17]{0,1:T(8,128)(4,1)S(1)} %copy-done.6, f32[128]{0:T(128)S(1)} %copy-done.2, bf16[4,3,3,3,128,128]{5,4,3,2,1,0:T(8,128)(2,1)} %param.6, bf16[26,8,1,7,2,128]{5,3,4,1,0,2:T(8,128)(2,1)S(1)} %slice.178, bf16[26,8,1,8,17,128]{5,3,4,1,0,2:T(8,128)(2,1)} %copy.46), kind=kOutput, calls=%fused_computation.52 | convolution fusion | flops 17373511680 | bytes 18900616 | tf_op jit(solution)/shard_map/conv_general_dilated | solution.py:26
  537.3 70.0 %psum.31 = f32[2,32]{1,0:T(2,128)S(1)} all-reduce(f32[2,32]{1,0:T(2,128)S(1)} %pad_maximum_fusion.11), channel_id=1, replica_groups=mesh['dp'=1,'hp'=2,'cp'=64] {'cp','hp'}, use_global_device_ids=true, to_apply=%region_19.20 | all-reduce | flops 64 | bytes 512 | tf_op jit(solution)/shard_map/psum | solution.py:15
  607.7 7.1 copy.47
  614.7 4.2 slice.179
  619.0 10.7 %multiply_convert_fusion = bf16[24,6,128,128]{3,1,2,0:T(8,128)(2,1)S(1)} fusion(f32[24,6,1,128,128]{4,0,3,1,2:T(8,128)} %slice.179, f32[128]{0:T(128)S(1)} %get-tuple-element.35, f32[128]{0:T(128)S(1)} %get-tuple-element.34, f32[128]{0:T(128)S(1)} %copy-done.2), kind=kLoop, calls=%fused_computation.43 | loop fusion | flops 23592960 | bytes 14157312 | tf_op jit(solution)/shard_map/convert_element_type | solution.py:22
  631.3 10.5 %collective-permute-done.9 = bf16[2,6,128,128]{3,1,2,0:T(8,128)(2,1)S(1)} collective-permute-done((bf16[2,6,128,128]{3,1,2,0:T(8,128)(2,1)S(1)}, bf16[2,6,128,128]{3,1,2,0:T(8,128)(2,1)S(1)}, u32[]{:S(2)}, u32[]{:S(2)}) %collective-permute-start.9) | collective-permute-done | bytes 393248 | tf_op jit(solution)/shard_map/ppermute | solution.py:47
  655.5 7.0 maximum_bitcast_fusion.3
  671.9 41.2 %broadcast_select_fusion = f32[24,6,8,17,128]{4,2,3,1,0:T(8,128)} fusion(pred[8,17]{0,1:T(8,128)(4,1)S(1)} %copy-done.6, bf16[26,8,1,7,2,128]{5,3,4,1,0,2:T(8,128)(2,1)S(1)} %slice.182, bf16[26,8,1,8,17,128]{5,3,4,1,0,2:T(8,128)(2,1)} %copy.54, bf16[4,3,3,3,128,128]{5,4,3,2,1,0:T(8,128)(2,1)} %param.6), kind=kOutput, calls=%fused_computation.85 | convolution fusion | flops 17353457664 | bytes 18899080 | tf_op jit(solution)/shard_map/conv_general_dilated | solution.py:26
  713.0 7.1 copy.55
  724.4 14.7 %fusion.21 = bf16[24,6,128,128]{3,1,2,0:T(8,128)(2,1)} fusion(bf16[24,6,128,128]{3,1,2,0:T(8,128)(2,1)} %get-tuple-element.17, f32[24,6,1,128,128]{4,0,3,1,2:T(8,128)} %slice.183, f32[128]{0:T(128)S(1)} %copy-done.1), kind=kLoop, calls=%fused_computation.30 | loop fusion | flops 14155776 | bytes 18874880 | tf_op jit(solution)/shard_map/convert_element_type | solution.py:55
  739.1 6.4 copy.57
  (133 shorter events, 106.6 us)
Async XLA Ops:
  83.9 2.7 copy-start
  86.6 12.5 %collective-permute-start = (bf16[2,6,128,128]{3,1,2,0:T(8,128)(2,1)S(1)}, bf16[2,6,128,128]{3,1,2,0:T(8,128)(2,1)S(1)}, u32[]{:S(2)}, u32[]{:S(2)}) collective-permute-start(bf16[2,6,128,128]{3,1,2,0:T(8,128)(2,1)S(1)} %slice.169), channel_id=1, source_target_pairs={{0,1},{1,2},{2,3},{3,4},{4,5},{5,6},{6,7},{7,8},{8,9},{9,10},{10,1... | collective-permute-start | bytes 1179656 | tf_op jit(solution)/shard_map/ppermute | solution.py:47
  89.6 22.3 %copy-start.3 = (f32[4,128]{1,0:T(4,128)S(1)}, f32[4,128]{1,0:T(4,128)}, u32[]{:S(2)}) copy-start(f32[4,128]{1,0:T(4,128)} %param.7) | copy-start | bytes 6148
  99.1 17.2 %slice-start = ((s8[6291456]{0:T(1024)(128)(4,1)}), s8[4194304]{0:T(1024)(128)(4,1)S(1)}, s32[]{:S(2)}) async-start(s8[6291456]{0:T(1024)(128)(4,1)} %bitcast.201), calls=%async_computation | async-start | bytes 8388608
  106.4 10.0 %slice-start.1 = ((s8[6291456]{0:T(1024)(128)(4,1)}), s8[2097152]{0:T(1024)(128)(4,1)S(1)}, s32[]{:S(2)}) async-start(s8[6291456]{0:T(1024)(128)(4,1)} %bitcast.201), calls=%async_computation.1 | async-start | bytes 4194304
  106.5 5.9 collective-permute-start.2
  110.4 4.3 collective-permute-start.1
  127.2 5.5 copy-start.6
  251.8 4.3 copy-start.4
  251.8 4.3 copy-start.5
  266.7 12.3 %collective-permute-start.3 = (bf16[2,6,128,128]{3,1,2,0:T(8,128)(2,1)S(1)}, bf16[2,6,128,128]{3,1,2,0:T(8,128)(2,1)S(1)}, u32[]{:S(2)}, u32[]{:S(2)}) collective-permute-start(bf16[2,6,128,128]{3,1,2,0:T(8,128)(2,1)S(1)} %slice.173), channel_id=1, source_target_pairs={{0,1},{1,2},{2,3},{3,4},{4,5},{5,6},{6,7},{7,8},{8,9},{9,10},{10,1... | collective-permute-start | bytes 1179656 | tf_op jit(solution)/shard_map/ppermute | solution.py:47
  283.1 5.4 collective-permute-start.5
  286.7 4.3 collective-permute-start.4
  303.6 58.0 %slice-start.2 = ((s8[4718592]{0:T(1024)(128)(4,1)}), s8[524288]{0:T(1024)(128)(4,1)S(1)}, s32[]{:S(2)}) async-start(s8[4718592]{0:T(1024)(128)(4,1)} %bitcast.203), calls=%async_computation.2 | async-start | bytes 1048576
  309.2 52.4 %slice-start.3 = ((s8[4718592]{0:T(1024)(128)(4,1)}), s8[4194304]{0:T(1024)(128)(4,1)S(1)}, s32[]{:S(2)}) async-start(s8[4718592]{0:T(1024)(128)(4,1)} %bitcast.203), calls=%async_computation.3 | async-start | bytes 8388608
  453.0 12.0 %collective-permute-start.6 = (bf16[2,6,128,128]{3,1,2,0:T(8,128)(2,1)S(1)}, bf16[2,6,128,128]{3,1,2,0:T(8,128)(2,1)S(1)}, u32[]{:S(2)}, u32[]{:S(2)}) collective-permute-start(bf16[2,6,128,128]{3,1,2,0:T(8,128)(2,1)S(1)} %slice.177), channel_id=1, source_target_pairs={{0,1},{1,2},{2,3},{3,4},{4,5},{5,6},{6,7},{7,8},{8,9},{9,10},{10,1... | collective-permute-start | bytes 1179656 | tf_op jit(solution)/shard_map/ppermute | solution.py:47
  469.1 5.4 collective-permute-start.8
  472.7 4.3 collective-permute-start.7
  489.8 5.5 copy-start.2
  629.7 12.2 %collective-permute-start.9 = (bf16[2,6,128,128]{3,1,2,0:T(8,128)(2,1)S(1)}, bf16[2,6,128,128]{3,1,2,0:T(8,128)(2,1)S(1)}, u32[]{:S(2)}, u32[]{:S(2)}) collective-permute-start(bf16[2,6,128,128]{3,1,2,0:T(8,128)(2,1)S(1)} %slice.181), channel_id=1, source_target_pairs={{0,1},{1,2},{2,3},{3,4},{4,5},{5,6},{6,7},{7,8},{8,9},{9,10},{10,1... | collective-permute-start | bytes 1179656 | tf_op jit(solution)/shard_map/ppermute | solution.py:47
  646.0 5.4 collective-permute-start.11
  649.6 4.3 collective-permute-start.10
  720.1 4.2 copy-start.1
where the time goes:
time: 759 us; the launch traced here: 746 us
  blocking collectives  278 us (37%)
  matrix products  165 us (22%)
  other arithmetic  120 us (16%)
  local copies, waits for them, and re-layouts  110 us (14%)
  waiting for transfers between devices  45.3 us (6%)
  starting transfers between devices  26.3 us (3%)
    psum x4, blocking collectives, norm_silu(): stat_sums = lax.psum(stat_sums, ('cp', 'hp'))  278 us
    conv_general_dilated x4, matrix products, conv_valid(): lax.conv_general_dilated(padded[None], kernel, (1, 1, 1), ((0, 0), (0, 0)...  165 us
    conv_general_dilated x16, local copies, waits for them, and re-layouts, conv_valid(): lax.conv_general_dilated(padded[None], kernel, (1, 1, 1), ((0, 0), (0, 0)...  67.3 us
    ppermute x4, waiting for transfers between devices, local_decode(): prev_frames = lax.ppermute(activated[frames - 2:], 'cp', time_fwd)  41.1 us
    convert_element_type x4, other arithmetic, norm_silu(): jax.nn.silu(local_act.astype(jnp.float32) * scale_c + shift_c)  33.4 us
    broadcast_in_dim x4, other arithmetic, conv_valid(): padded[None]  28.6 us
    reduce_sum x6, other arithmetic, norm_silu(): jnp.sum(grouped, axis=(0, 1, 2, 4))  22.7 us
    slice x4, other arithmetic, local_decode(): from_above = lax.ppermute(extended[:, row_count - 1:], 'hp', rows_down)  19 us
  transfers between devices with their start and end apart: 12, of which 11 were waited for; matrix products, arithmetic and copies ran while one was open for 1% of the time, Pallas kernels for 0%

commit v1 on v0

v1 whole, which is shorter than its diff:
```python
import functools

import jax
import jax.numpy as jnp
from jax import lax
from jax.experimental import pallas as pl
from jax.experimental.pallas import tpu as pltpu
from jax.sharding import PartitionSpec as P

MESH = pl.DeviceIdType.MESH
GROUPS = 32
EPS = 1e-6
FRAMES = 24
ROWS = 6
W = 128
C = 128
TRIPS = 4
CHUNKS = ((22, 4), (16, 6), (10, 6), (4, 6), (2, 2))
SIDE = 64
BF = jnp.bfloat16
F32 = jnp.float32


def kernel(count, n_cp, lat, w_hbm, bias, gamma, beta, out, buf_a, buf_b, act0, act1, act2, wts, tmp, stat_out, stat_in,
           x_sem, w_sem, out_sem, row_send, row_recv, frame_send, frame_recv, stat_send, stat_recv):
    me = lax.axis_index("cp")
    hp = lax.axis_index("hp")
    acts = (act0, act1, act2)
    cx, cy, cz = me % 4, (me // 4) % 4, me // 16
    partner = {"hp": 1 - hp}
    after = {"cp": (me + 1) % n_cp}
    before = {"cp": (me + n_cp - 1) % n_cp}

    def at(x, y, z):
        return (z * 4 + y) * 4 + x

    ring = (2, 1, 3)
    x_peers = [((cx + d) % 4, h) for d in ring for h in (0, 1)]
    y_peers = [(cy + d) % 4 for d in ring]
    z_peers = [(cz + d) % 4 for d in ring]

    def x_load(c):
        f, n = CHUNKS[c]
        return pltpu.make_async_copy(lat.at[pl.ds(f - 2, n)], buf_a.at[pl.ds(f, n), pl.ds(0, ROWS)], x_sem.at[c])

    def w_load(l):
        return pltpu.make_async_copy(w_hbm.at[l], wts.at[l], w_sem.at[l])

    for c in range(5):
        x_load(c).start()
    for l in range(4):
        w_load(l).start()

    barrier = pltpu.get_barrier_semaphore()
    greet = [partner, after, before]
    greet += [{"cp": at(x, cy, cz), "hp": h} for x, h in x_peers]
    greet += [{"cp": at(cx, y, cz)} for y in y_peers]
    greet += [{"cp": at(cx, cy, z)} for z in z_peers]
    for d in greet:
        pl.semaphore_signal(barrier, inc=1, device_id=d, device_id_type=MESH)

    def row_copy(s, c):
        buf = (buf_a, buf_b)[s % 2]
        f, n = CHUNKS[c]
        edge = (ROWS - 1) * (1 - hp)
        return pltpu.make_async_remote_copy(
            src_ref=buf.at[pl.ds(f, n), pl.ds(edge, 1)], dst_ref=buf.at[pl.ds(f, n), pl.ds(ROWS, 1)],
            send_sem=row_send.at[s, c], recv_sem=row_recv.at[s, c], device_id=partner, device_id_type=MESH)

    def frame_copy(s):
        buf = (buf_a, buf_b)[s % 2]
        return pltpu.make_async_remote_copy(
            src_ref=buf.at[pl.ds(24, 2)], dst_ref=buf.at[pl.ds(0, 2)],
            send_sem=frame_send.at[s], recv_sem=frame_recv.at[s], device_id=after, device_id_type=MESH)

    def out_copy(c):
        f, n = CHUNKS[c]
        return pltpu.make_async_copy(buf_a.at[pl.ds(f, n), pl.ds(0, ROWS)], out.at[pl.ds(f - 2, n)], out_sem.at[c])

    def stat_copy(s, k, src, slot, device):
        return pltpu.make_async_remote_copy(
            src_ref=stat_out.at[s, src], dst_ref=stat_in.at[s, slot],
            send_sem=stat_send.at[s, k], recv_sem=stat_recv.at[s, slot], device_id=device, device_id_type=MESH)

    row_id = lax.broadcasted_iota(jnp.int32, (8, C), 0)
    lane_id = lax.broadcasted_iota(jnp.int32, (8, C), 1)

    def reduce_stats(s, s1, s2, mid):
        v1 = jnp.sum(s1, axis=0, keepdims=True)
        v2 = jnp.sum(s2, axis=0, keepdims=True)
        part = jnp.where(row_id == 0, v1, jnp.where(row_id == 1, v2, 0.0))
        phases = (
            (cx * 2 + hp, 0, 8, [(x * 2 + h, {"cp": at(x, cy, cz), "hp": h}) for x, h in x_peers] + [(cx * 2 + 1 - hp, partner)]),
            (cy, 8, 4, [(y, {"cp": at(cx, y, cz)}) for y in y_peers]),
            (cz, 12, 4, [(z, {"cp": at(cx, cy, z)}) for z in z_peers]),
        )
        k = 0
        sends = []
        for ph, (own, base, n, peers) in enumerate(phases):
            stat_out[s, ph] = part
            stat_in[s, base + own] = part
            first = k
            for _, device in peers:
                c = stat_copy(s, k, ph, base + own, device)
                c.start()
                sends.append(c)
                k += 1
            if ph == 0:
                mid()
            for i, (slot, device) in enumerate(peers):
                stat_copy(s, first + i, ph, base + slot, device).wait_recv()
            part = stat_in[s, base]
            for i in range(1, n):
                part = part + stat_in[s, base + i]
        for c in sends:
            c.wait_send()
        return part

    def coefficients(l, part):
        pair = part + jnp.where(lane_id % 2 == 0, pltpu.roll(part, C - 1, 1), pltpu.roll(part, 1, 1))
        group = pair + jnp.where(lane_id % 4 < 2, pltpu.roll(pair, C - 2, 1), pltpu.roll(pair, 2, 1))
        mean = group[0:1] / count
        var = group[1:2] / count - mean * mean
        inv = lax.rsqrt(var + EPS)
        g = gamma[l:l + 1]
        scale = inv * g
        shift = beta[l:l + 1] - mean * inv * g
        return jnp.broadcast_to(0.5 * scale, (8, C)), jnp.broadcast_to(0.5 * shift, (8, C))

    col8 = lax.broadcasted_iota(jnp.int32, (W, C), 0)
    halo_row = 7 * (1 - hp)

    def norm_row(src, dst, q, e, r, coef):
        scale, shift = coef
        f = jnp.maximum(24 - 2 * q, 0) + e
        f = jnp.where((q >= 12) & (me == 0), 2, f)
        v = src[f, r].astype(F32).reshape(W // 8, 8, C)
        u = (v * scale[None] + shift[None]).reshape(W, C)
        a = u + u * jnp.tanh(u)
        row = halo_row if r == ROWS else r + 1
        dst[1, e, row] = a.astype(BF)
        dst[0, e, row] = jnp.where(col8 == 0, 0.0, pltpu.roll(a, 1, 0)).astype(BF)
        dst[2, e, row] = jnp.where(col8 == W - 1, 0.0, pltpu.roll(a, W - 1, 0)).astype(BF)

    def tile(l, n, m):
        def w(k, di, dj):
            return wts[l, k * 9 + di * 3 + dj]

        def block(a, b, c, d):
            return jnp.concatenate([jnp.concatenate([a, b], 1), jnp.concatenate([c, d], 1)], 0)

        if n < 9:
            di, dj = n // 3, n % 3
            return block(w(1, di, dj), w(0, di, dj), w(2, di, dj), w(1, di, dj))
        dj, half = (n - 9) % 3, (n - 9) // 3
        k = 0 if m == 0 else 2
        if half == 0:
            return block(w(k, 1, dj), w(k, 0, dj), w(k, 2, dj), w(k, 1, dj))
        zero = jnp.zeros((C, C), BF)
        return block(w(k, 0, dj), zero, zero, w(k, 2, dj))

    def lhs(cur, prv, n, m, j):
        if n < 9:
            di, dj = n // 3, n % 3
            i = 3 * m + j + di
            return jnp.concatenate([prv[dj, 1, i], cur[dj, 0, i]], 1)
        dj, half = (n - 9) % 3, (n - 9) // 3
        frame = prv.at[dj, 0] if m == 0 else cur.at[dj, 1]
        i = 2 * j
        if half == 0:
            return jnp.concatenate([frame[i + 1], frame[i + 2]], 1)
        return jnp.concatenate([frame[i], frame[i + 3]], 1)

    def sum8(v):
        return jnp.sum(v.reshape(W // 8, 8, C), axis=0)

    def layer(l, coef):
        src = (buf_a, buf_b)[l % 2]
        dst = (buf_a, buf_b)[1 - l % 2]
        residual = l % 2 == 1
        last = l == 3
        bias2 = jnp.concatenate([bias[l:l + 1], bias[l:l + 1]], 1)

        def finish(q, e, j, full, v, sums):
            f = 24 - 2 * q + e
            s1, s2 = sums
            for half in range(2):
                o = 2 * j + half
                h = (full[o * W:(o + 1) * W, e * C:(e + 1) * C] + v[j * W:(j + 1) * W, half * C:(half + 1) * C]).astype(BF)
                if residual:
                    h = (dst[f, o].astype(F32) + h.astype(F32)).astype(BF)
                dst[f, o] = h
                if not last:
                    hf = h.astype(F32)
                    s1 = s1 + sum8(hf)
                    s2 = s2 + sum8(hf * hf)
            return s1, s2

        def trip(it, sums):
            def wait_rows(c):
                row_copy(l, c).wait_recv()

            for i in range(3):
                @pl.when(it == i)
                def _(i=i):
                    wait_rows(i + 1)

            @pl.when(it == 3)
            def _():
                wait_rows(4)
                frame_copy(l).wait_recv()

            for i in range(1, 4):
                @pl.when(it == i)
                def _(i=i):
                    if last:
                        out_copy(i - 1).start()
                    else:
                        row_copy(l + 1, i - 1).start()
                        if i == 2:
                            row_copy(l + 1, 0).wait_recv()
                            frame_copy(l + 1).start()

            for k in range(3):
                q = 3 * it + k
                cur, prv, nxt = acts[k], acts[(k + 1) % 3], acts[(k + 2) % 3]
                full = jnp.dot(
                    jnp.concatenate([jnp.concatenate([lhs(cur, prv, n, m, j) for n in range(9)], 1) for m in range(2) for j in range(3)], 0),
                    jnp.concatenate([tile(l, n, 0) for n in range(9)], 0), preferred_element_type=F32) + bias2
                half = [jnp.dot(
                    jnp.concatenate([jnp.concatenate([lhs(cur, prv, n, m, j) for n in range(9, 15)], 1) for j in range(3)], 0),
                    jnp.concatenate([tile(l, n, m) for n in range(9, 15)], 0), preferred_element_type=F32) for m in range(2)]
                for e in range(2):
                    for r in range(7):
                        norm_row(src, nxt, q + 2, e, r, coef)
                for e in range(2):
                    for j in range(3):
                        sums = finish(q, e, j, full, half[e], sums)
            return sums

        for q in range(2):
            for e in range(2):
                for r in range(7):
                    norm_row(src, acts[q], q, e, r, coef)
        zero = jnp.zeros((8, C), F32)
        sums = lax.fori_loop(0, TRIPS, trip, (zero, zero))
        if last:
            out_copy(3).start()
        else:
            row_copy(l + 1, 3).start()
        for c in range(5):
            row_copy(l, c).wait_send()
        frame_copy(l).wait_send()
        if last:
            out_copy(4).start()
        return sums

    def body():
        blank = jnp.zeros((W, C), BF)
        for act in acts:
            for dj in range(3):
                for e in range(2):
                    for r in (0, 7):
                        act[dj, e, r] = blank

        sums = (jnp.zeros((8, C), F32), jnp.zeros((8, C), F32))
        for c, (f, n) in enumerate(CHUNKS):
            x_load(c).wait()

            def add(i, sums, f=f):
                s1, s2 = sums
                for r in range(ROWS):
                    v = buf_a[f + i, r].astype(F32)
                    s1 = s1 + sum8(v)
                    s2 = s2 + sum8(v * v)
                return s1, s2

            sums = lax.fori_loop(0, n, add, sums)

        pl.semaphore_wait(barrier, len(greet))
        for l in range(4):
            w_load(l).wait()
        for l in range(4):
            def mid(l=l):
                if l == 0:
                    for c in range(5):
                        row_copy(0, c).start()
                    row_copy(0, 0).wait_recv()
                    frame_copy(0).start()
                else:
                    row_copy(l, 4).start()

            part = reduce_stats(l, *sums, mid)
            sums = layer(l, coefficients(l, part))
        for c in range(5):
            out_copy(c).wait()

    body()


def solution(mesh):
    n_cp, n_hp = mesh.shape["cp"], mesh.shape["hp"]

    def local(lat, conv_w, conv_b, gn_gamma, gn_beta):
        count = float(FRAMES * n_cp * ROWS * n_hp * W * (C // GROUPS))
        any_spec = pl.BlockSpec(memory_space=pl.ANY)
        vmem = pl.BlockSpec(memory_space=pltpu.VMEM)
        dma = pltpu.SemaphoreType.DMA
        return pl.pallas_call(
            functools.partial(kernel, count, n_cp),
            out_shape=jax.ShapeDtypeStruct((FRAMES, ROWS, W, C), BF),
            in_specs=[any_spec, any_spec, vmem, vmem, vmem],
            out_specs=any_spec,
            scratch_shapes=[
                pltpu.VMEM((FRAMES + 4, ROWS + 1, W, C), BF),
                pltpu.VMEM((FRAMES + 4, ROWS + 1, W, C), BF),
                pltpu.VMEM((3, 2, ROWS + 2, W, C), BF),
                pltpu.VMEM((3, 2, ROWS + 2, W, C), BF),
                pltpu.VMEM((3, 2, ROWS + 2, W, C), BF),
                pltpu.VMEM((4, 27, C, C), BF),
                pltpu.VMEM((ROWS, W, 2 * C), F32),
                pltpu.VMEM((4, 3, 8, C), F32),
                pltpu.VMEM((4, 16, 8, C), F32),
                dma((5,)), dma((4,)), dma((5,)),
                dma((4, 5)), dma((4, 5)), dma((4,)), dma((4,)),
                dma((4, 13)), dma((4, 16)),
            ],
            compiler_params=pltpu.CompilerParams(collective_id=0, has_side_effects=True, vmem_limit_bytes=60 * 2**20),
        )(lat, conv_w.reshape(4, 27, C, C), conv_b, gn_gamma, gn_beta)

    video = P(("dp", "cp"), "hp", None, None)
    return jax.shard_map(local, mesh=mesh, in_specs=(video, P(), P(), P(), P()), out_specs=video, check_vma=False)
```

time: 759 us -> 154 us (0.20); the launches traced: 746 us -> 153 us
  blocking collectives: 278 us -> 0 us
  matrix products: 165 us -> 0 us
  Pallas kernels: 0 us -> 146 us
  other arithmetic: 120 us -> 0 us
  local copies, waits for them, and re-layouts: 110 us -> 6.36 us
  waiting for transfers between devices: 45.3 us -> 0 us
  starting transfers between devices: 26.3 us -> 0 us
    psum x4 -> x0, blocking collectives: 278 us -> none  [norm_silu(): stat_sums = lax.psum(stat_sums, ('cp', 'hp'))]
    conv_general_dilated x4 -> x0, matrix products: 165 us -> none  [conv_valid(): lax.conv_general_dilated(padded[None], kernel, (1, 1, 1), ((0, 0), (0, 0)...]
    pallas_call x0 -> x1, Pallas kernels: none -> 146 us  [local(): pl.pallas_call(functools.partial(kernel, count, n_cp), out_shape=jax.Shap...]
    conv_general_dilated x16 -> x0, local copies, waits for them, and re-layouts: 67.3 us -> none  [conv_valid(): lax.conv_general_dilated(padded[None], kernel, (1, 1, 1), ((0, 0), (0, 0)...]
    convert_element_type x5 -> x0, other arithmetic: 48 us -> none  [the longest x4 33.4 us: norm_silu(): jax.nn.silu(local_act.astype(jnp.float32) * scale_c + shift_c)]
    ppermute x12 -> x0, waiting for transfers between devices: 45.3 us -> none  [the longest x4 41.1 us: local_decode(): prev_frames = lax.ppermute(activated[frames - 2:], 'cp', time_fwd)]
    broadcast_in_dim x4 -> x0, other arithmetic: 28.6 us -> none  [conv_valid(): padded[None]]
    ppermute x12 -> x0, starting transfers between devices: 26.3 us -> none  [the longest x4 14 us: local_decode(): from_below = lax.ppermute(extended[:, :1], 'hp', rows_up)]
  transfers between devices with their start and end apart: 12 -> 0, of which waited for: 11 -> 0; matrix products, arithmetic and copies ran while one was open for 1% -> 0% of each run, Pallas kernels for 0% -> 0%
where the time goes in v1:
time: 154 us; the launch traced here: 153 us
  Pallas kernels  146 us (95%)
  local copies, waits for them, and re-layouts  6.36 us (4%)
    pallas_call x1, Pallas kernels, local(): pl.pallas_call(functools.partial(kernel, count, n_cp), out_shape=jax.Shap...  146 us
    unnamed x1, local copies, waits for them, and re-layouts  6.36 us

profile of v1, /device:TPU:1, one launch (start us, length us, event | category | flops | bytes accessed | tf_op | source)
XLA Modules:
  0.0 152.7 jit_solution(7409167833307171684)
XLA Ops:
  0.0 146.3 %shard_map.55 = bf16[24,6,128,128]{3,2,1,0:T(8,128)(2,1)} custom-call(bf16[24,6,128,128]{3,2,1,0:T(8,128)(2,1)} %lat.1, bf16[4,27,128,128]{3,2,1,0:T(8,128)(2,1)} %bitcast.1, f32[4,128]{1,0:T(4,128)} %bias.1, f32[4,128]{1,0:T(4,128)} %gamma.1, f32[4,128]{1,0:T(4,128)} %beta.1), custom_call_target="tpu_custom_call" | custom-call | tf_op jit(solution)/shard_map/pallas_call | solution.py:309
  146.3 6.4 %copy.7 = bf16[24,6,128,128]{3,2,1,0:T(8,128)(2,1)} copy(bf16[24,6,128,128]{3,2,1,0:T(8,128)(2,1)} %shard_map.55) | data formatting | bytes 9437184

commit v2 on v1

--- a/solution.py
+++ b/solution.py
@@ -21,23 +21,16 @@
 F32 = jnp.float32
 
 
-def kernel(count, n_cp, lat, w_hbm, bias, gamma, beta, out, buf_a, buf_b, act0, act1, act2, wts, tmp, stat_out, stat_in,
+def kernel(count, n_cp, lat, w_hbm, bias, gamma, beta, out, buf_a, buf_b, act0, act1, act2, wts, stat_out, stat_in,
            x_sem, w_sem, out_sem, row_send, row_recv, frame_send, frame_recv, stat_send, stat_recv):
     me = lax.axis_index("cp")
     hp = lax.axis_index("hp")
     acts = (act0, act1, act2)
-    cx, cy, cz = me % 4, (me // 4) % 4, me // 16
     partner = {"hp": 1 - hp}
     after = {"cp": (me + 1) % n_cp}
-    before = {"cp": (me + n_cp - 1) % n_cp}
-
-    def at(x, y, z):
-        return (z * 4 + y) * 4 + x
-
-    ring = (2, 1, 3)
-    x_peers = [((cx + d) % 4, h) for d in ring for h in (0, 1)]
-    y_peers = [(cy + d) % 4 for d in ring]
-    z_peers = [(cz + d) % 4 for d in ring]
+
+    def peer(j):
+        return (me + 1 + (j + n_cp // 2 - 1) % (n_cp - 1)) % n_cp
 
     def x_load(c):
         f, n = CHUNKS[c]
@@ -52,12 +45,12 @@
         w_load(l).start()
 
     barrier = pltpu.get_barrier_semaphore()
-    greet = [partner, after, before]
-    greet += [{"cp": at(x, cy, cz), "hp": h} for x, h in x_peers]
-    greet += [{"cp": at(cx, y, cz)} for y in y_peers]
-    greet += [{"cp": at(cx, cy, z)} for z in z_peers]
-    for d in greet:
-        pl.semaphore_signal(barrier, inc=1, device_id=d, device_id_type=MESH)
+    def greet(j, _):
+        pl.semaphore_signal(barrier, inc=1, device_id={"cp": peer(j)}, device_id_type=MESH)
+        return _
+
+    pl.semaphore_signal(barrier, inc=1, device_id=partner, device_id_type=MESH)
+    lax.fori_loop(0, n_cp - 1, greet, 0)
 
     def row_copy(s, c):
         buf = (buf_a, buf_b)[s % 2]
@@ -77,46 +70,47 @@
         f, n = CHUNKS[c]
         return pltpu.make_async_copy(buf_a.at[pl.ds(f, n), pl.ds(0, ROWS)], out.at[pl.ds(f - 2, n)], out_sem.at[c])
 
-    def stat_copy(s, k, src, slot, device):
+    def chip_copy(s, j, slot):
+        p = peer(j)
         return pltpu.make_async_remote_copy(
-            src_ref=stat_out.at[s, src], dst_ref=stat_in.at[s, slot],
-            send_sem=stat_send.at[s, k], recv_sem=stat_recv.at[s, slot], device_id=device, device_id_type=MESH)
+            src_ref=stat_out.at[s % 2, 0], dst_ref=stat_in.at[s % 2, p if slot is None else slot],
+            send_sem=stat_send.at[s % 2, p], recv_sem=stat_recv.at[s % 2, p if slot is None else slot],
+            device_id={"cp": p}, device_id_type=MESH)
+
+    def core_copy(s):
+        return pltpu.make_async_remote_copy(
+            src_ref=stat_out.at[s % 2, 1], dst_ref=stat_in.at[s % 2, n_cp], send_sem=stat_send.at[s % 2, n_cp],
+            recv_sem=stat_recv.at[s % 2, n_cp], device_id=partner, device_id_type=MESH)
 
     row_id = lax.broadcasted_iota(jnp.int32, (8, C), 0)
     lane_id = lax.broadcasted_iota(jnp.int32, (8, C), 1)
 
     def reduce_stats(s, s1, s2, mid):
-        v1 = jnp.sum(s1, axis=0, keepdims=True)
-        v2 = jnp.sum(s2, axis=0, keepdims=True)
-        part = jnp.where(row_id == 0, v1, jnp.where(row_id == 1, v2, 0.0))
-        phases = (
-            (cx * 2 + hp, 0, 8, [(x * 2 + h, {"cp": at(x, cy, cz), "hp": h}) for x, h in x_peers] + [(cx * 2 + 1 - hp, partner)]),
-            (cy, 8, 4, [(y, {"cp": at(cx, y, cz)}) for y in y_peers]),
-            (cz, 12, 4, [(z, {"cp": at(cx, cy, z)}) for z in z_peers]),
-        )
-        k = 0
-        sends = []
-        for ph, (own, base, n, peers) in enumerate(phases):
-            stat_out[s, ph] = part
-            stat_in[s, base + own] = part
-            first = k
-            for _, device in peers:
-                c = stat_copy(s, k, ph, base + own, device)
-                c.start()
-                sends.append(c)
-                k += 1
-            if ph == 0:
-                mid()
-            for i, (slot, device) in enumerate(peers):
-                stat_copy(s, first + i, ph, base + slot, device).wait_recv()
-            part = stat_in[s, base]
-            for i in range(1, n):
-                part = part + stat_in[s, base + i]
-        for c in sends:
-            c.wait_send()
-        return part
+        part = jnp.concatenate([jnp.sum(s1, axis=0, keepdims=True), jnp.sum(s2, axis=0, keepdims=True)], 0)
+        stat_out[s % 2, 0] = part
+        stat_in[s % 2, me] = part
+
+        def send(j, _):
+            chip_copy(s, j, me).start()
+            return _
+
+        def wait(j, _):
+            chip_copy(s, j, None).wait()
+            return _
+
+        lax.fori_loop(0, n_cp - 1, send, 0)
+        mid()
+        lax.fori_loop(0, n_cp - 1, wait, 0)
+        terms = [stat_in[s % 2, i] for i in range(n_cp)]
+        while len(terms) > 1:
+            terms = [a + b for a, b in zip(terms[::2], terms[1::2])]
+        stat_out[s % 2, 1] = terms[0]
+        core_copy(s).start()
+        core_copy(s).wait()
+        return terms[0] + stat_in[s % 2, n_cp]
 
     def coefficients(l, part):
+        part = jnp.where(row_id == 0, part[0:1], part[1:2])
         pair = part + jnp.where(lane_id % 2 == 0, pltpu.roll(part, C - 1, 1), pltpu.roll(part, 1, 1))
         group = pair + jnp.where(lane_id % 4 < 2, pltpu.roll(pair, C - 2, 1), pltpu.roll(pair, 2, 1))
         mean = group[0:1] / count
@@ -277,20 +271,20 @@
 
             sums = lax.fori_loop(0, n, add, sums)
 
-        pl.semaphore_wait(barrier, len(greet))
-        for l in range(4):
-            w_load(l).wait()
+        pl.semaphore_wait(barrier, n_cp)
         for l in range(4):
             def mid(l=l):
                 if l == 0:
                     for c in range(5):
                         row_copy(0, c).start()
-                    row_copy(0, 0).wait_recv()
-                    frame_copy(0).start()
                 else:
                     row_copy(l, 4).start()
 
             part = reduce_stats(l, *sums, mid)
+            w_load(l).wait()
+            if l == 0:
+                row_copy(0, 0).wait_recv()
+                frame_copy(0).start()
             sums = layer(l, coefficients(l, part))
         for c in range(5):
             out_copy(c).wait()
@@ -318,12 +312,11 @@
                 pltpu.VMEM((3, 2, ROWS + 2, W, C), BF),
                 pltpu.VMEM((3, 2, ROWS + 2, W, C), BF),
                 pltpu.VMEM((4, 27, C, C), BF),
-                pltpu.VMEM((ROWS, W, 2 * C), F32),
-                pltpu.VMEM((4, 3, 8, C), F32),
-                pltpu.VMEM((4, 16, 8, C), F32),
+                pltpu.VMEM((2, 2, 2, C), F32),
+                pltpu.VMEM((2, n_cp + 1, 2, C), F32),
                 dma((5,)), dma((4,)), dma((5,)),
                 dma((4, 5)), dma((4, 5)), dma((4,)), dma((4,)),
-                dma((4, 13)), dma((4, 16)),
+                dma((2, n_cp + 1)), dma((2, n_cp + 1)),
             ],
             compiler_params=pltpu.CompilerParams(collective_id=0, has_side_effects=True, vmem_limit_bytes=60 * 2**20),
         )(lat, conv_w.reshape(4, 27, C, C), conv_b, gn_gamma, gn_beta)

time: 154 us -> 146 us (0.948)
  Pallas kernels: 146 us -> 139 us
    pallas_call x1, Pallas kernels: 146 us -> 139 us  [local(): pl.pallas_call(functools.partial(kernel, count, n_cp), out_shape=jax.Shap...]
where the time goes in v2:
time: 146 us
  Pallas kernels  139 us (95%)
  local copies, waits for them, and re-layouts  6.36 us (4%)
    pallas_call x1, Pallas kernels, local(): pl.pallas_call(functools.partial(kernel, count, n_cp), out_shape=jax.Shap...  139 us
    unnamed x1, local copies, waits for them, and re-layouts  6.36 us

profile of v2, /device:TPU:1, one launch (start us, length us, event | category | flops | bytes accessed | tf_op | source)
XLA Modules:
  0.0 145.8 jit_solution(14827723557628440569)
XLA Ops:
  0.0 139.5 %shard_map.55 = bf16[24,6,128,128]{3,2,1,0:T(8,128)(2,1)} custom-call(bf16[24,6,128,128]{3,2,1,0:T(8,128)(2,1)} %lat.1, bf16[4,27,128,128]{3,2,1,0:T(8,128)(2,1)} %bitcast.1, f32[4,128]{1,0:T(4,128)} %bias.1, f32[4,128]{1,0:T(4,128)} %gamma.1, f32[4,128]{1,0:T(4,128)} %beta.1), custom_call_target="tpu_custom_call" | custom-call | tf_op jit(solution)/shard_map/pallas_call | solution.py:303
  139.5 6.4 %copy.7 = bf16[24,6,128,128]{3,2,1,0:T(8,128)(2,1)} copy(bf16[24,6,128,128]{3,2,1,0:T(8,128)(2,1)} %shard_map.55) | data formatting | bytes 9437184

commit v3 on v2

--- a/solution.py
+++ b/solution.py
@@ -29,8 +29,15 @@
     partner = {"hp": 1 - hp}
     after = {"cp": (me + 1) % n_cp}
 
-    def peer(j):
-        return (me + 1 + (j + n_cp // 2 - 1) % (n_cp - 1)) % n_cp
+    half = n_cp // 2
+
+    def outward(step):
+        lax.fori_loop(0, half, lambda j, n: step((me + half + j) % n_cp, n), 0)
+        lax.fori_loop(1, half, lambda j, n: step((me + j) % n_cp, n), 0)
+
+    def inward(step):
+        lax.fori_loop(1, half, lambda j, n: step((me + j) % n_cp, n), 0)
+        lax.fori_loop(0, half, lambda j, n: step((me + n_cp - 1 - j) % n_cp, n), 0)
 
     def x_load(c):
         f, n = CHUNKS[c]
@@ -45,12 +52,12 @@
         w_load(l).start()
 
     barrier = pltpu.get_barrier_semaphore()
-    def greet(j, _):
-        pl.semaphore_signal(barrier, inc=1, device_id={"cp": peer(j)}, device_id_type=MESH)
-        return _
+    def greet(p, n):
+        pl.semaphore_signal(barrier, inc=1, device_id={"cp": p}, device_id_type=MESH)
+        return n
 
     pl.semaphore_signal(barrier, inc=1, device_id=partner, device_id_type=MESH)
-    lax.fori_loop(0, n_cp - 1, greet, 0)
+    outward(greet)
 
     def row_copy(s, c):
         buf = (buf_a, buf_b)[s % 2]
@@ -70,12 +77,10 @@
         f, n = CHUNKS[c]
         return pltpu.make_async_copy(buf_a.at[pl.ds(f, n), pl.ds(0, ROWS)], out.at[pl.ds(f - 2, n)], out_sem.at[c])
 
-    def chip_copy(s, j, slot):
-        p = peer(j)
+    def chip_copy(s, p, slot):
         return pltpu.make_async_remote_copy(
-            src_ref=stat_out.at[s % 2, 0], dst_ref=stat_in.at[s % 2, p if slot is None else slot],
-            send_sem=stat_send.at[s % 2, p], recv_sem=stat_recv.at[s % 2, p if slot is None else slot],
-            device_id={"cp": p}, device_id_type=MESH)
+            src_ref=stat_out.at[s % 2, 0], dst_ref=stat_in.at[s % 2, slot], send_sem=stat_send.at[s % 2, p],
+            recv_sem=stat_recv.at[s % 2, slot], device_id={"cp": p}, device_id_type=MESH)
 
     def core_copy(s):
         return pltpu.make_async_remote_copy(
@@ -90,17 +95,22 @@
         stat_out[s % 2, 0] = part
         stat_in[s % 2, me] = part
 
-        def send(j, _):
-            chip_copy(s, j, me).start()
-            return _
-
-        def wait(j, _):
-            chip_copy(s, j, None).wait()
-            return _
-
-        lax.fori_loop(0, n_cp - 1, send, 0)
+        def send(p, n):
+            chip_copy(s, p, me).start()
+            return n
+
+        def sent(p, n):
+            chip_copy(s, p, p).wait_send()
+            return n
+
+        def landed(p, n):
+            chip_copy(s, p, p).wait_recv()
+            return n
+
+        outward(send)
         mid()
-        lax.fori_loop(0, n_cp - 1, wait, 0)
+        outward(sent)
+        inward(landed)
         terms = [stat_in[s % 2, i] for i in range(n_cp)]
         while len(terms) > 1:
             terms = [a + b for a, b in zip(terms[::2], terms[1::2])]
@@ -292,6 +302,10 @@
     body()
 
 
+def hand_over(src, dst):
+    dst[...] = src[...]
+
+
 def solution(mesh):
     n_cp, n_hp = mesh.shape["cp"], mesh.shape["hp"]
 
@@ -300,7 +314,7 @@
         any_spec = pl.BlockSpec(memory_space=pl.ANY)
         vmem = pl.BlockSpec(memory_space=pltpu.VMEM)
         dma = pltpu.SemaphoreType.DMA
-        return pl.pallas_call(
+        decoded = pl.pallas_call(
             functools.partial(kernel, count, n_cp),
             out_shape=jax.ShapeDtypeStruct((FRAMES, ROWS, W, C), BF),
             in_specs=[any_spec, any_spec, vmem, vmem, vmem],
@@ -320,6 +334,10 @@
             ],
             compiler_params=pltpu.CompilerParams(collective_id=0, has_side_effects=True, vmem_limit_bytes=60 * 2**20),
         )(lat, conv_w.reshape(4, 27, C, C), conv_b, gn_gamma, gn_beta)
+        block = pl.BlockSpec((3, ROWS, W, C), lambda i: (i, 0, 0, 0))
+        return pl.pallas_call(
+            hand_over, grid=(FRAMES // 3,), out_shape=jax.ShapeDtypeStruct((FRAMES, ROWS, W, C), BF),
+            in_specs=[block], out_specs=block)(decoded)
 
     video = P(("dp", "cp"), "hp", None, None)
     return jax.shard_map(local, mesh=mesh, in_specs=(video, P(), P(), P(), P()), out_specs=video, check_vma=False)

time: 146 us -> 140 us (0.959)
  local copies, waits for them, and re-layouts: 6.36 us -> 0 us
    pallas_call x0 -> x1, Pallas kernels: none -> 6.82 us  [local(): pl.pallas_call(hand_over, grid=(FRAMES // 3,), out_shape=jax.ShapeDtypeSt...]
    pallas_call x1, Pallas kernels: 139 us -> 133 us  [local(): pl.pallas_call(functools.partial(kernel, count, n_cp), out_shape=jax.Shap...]
    unnamed x1 -> x0, local copies, waits for them, and re-layouts: 6.36 us -> none
where the time goes in v3:
time: 140 us
  Pallas kernels  140 us (100%)
    pallas_call x1, Pallas kernels, local(): pl.pallas_call(functools.partial(kernel, count, n_cp), out_shape=jax.Shap...  133 us
    pallas_call x1, Pallas kernels, local(): pl.pallas_call(hand_over, grid=(FRAMES // 3,), out_shape=jax.ShapeDtypeSt...  6.82 us

profile of v3, /device:TPU:1, one launch (start us, length us, event | category | flops | bytes accessed | tf_op | source)
XLA Modules:
  0.0 139.8 jit_solution(8338005323790215572)
XLA Ops:
  0.0 132.9 %shard_map.55.src = bf16[24,6,128,128]{3,2,1,0:T(8,128)(2,1)} custom-call(bf16[24,6,128,128]{3,2,1,0:T(8,128)(2,1)} %lat.1, bf16[4,27,128,128]{3,2,1,0:T(8,128)(2,1)} %bitcast.1, f32[4,128]{1,0:T(4,128)} %bias.1, f32[4,128]{1,0:T(4,128)} %gamma.1, f32[4,128]{1,0:T(4,128)} %beta.1), custom_call_target="tpu_custom_call" | custom-call | tf_op jit(solution)/shard_map/pallas_call | solution.py:317
  133.0 6.8 %shard_map.56 = bf16[24,6,128,128]{3,2,1,0:T(8,128)(2,1)} custom-call(bf16[24,6,128,128]{3,2,1,0:T(8,128)(2,1)} %shard_map.55.src), custom_call_target="tpu_custom_call" | custom-call | tf_op jit(solution)/shard_map/pallas_call | solution.py:338
